TPU v7x, 32 devices: a whole 2x2x4 slice. The times are simulated.
32 devices in a mesh: cuts: 4 (over z), dp: 4 (over y, x), mp: 2 (over core).
Axes of the slice: x: 2, y: 2, z: 4, core: 2. Of those that a mesh axis runs over, the one named last changes fastest.
Arguments:
- attn_out: bfloat16 [2048, 3072], P(('cuts', 'dp'), 'mp'), may hold values from -6 to 6
- out_weight: bfloat16 [3072, 6144], P('mp'), may hold values from -0.109375 to 0.109375
- residual: bfloat16 [2048, 6144], P(('cuts', 'dp', 'mp')), may hold values from -45 to 45
- target: bfloat16 [2048, 6144], P(('cuts', 'dp', 'mp')), may hold values from -5 to 5
- norm_gain: float32 [6144], replicated, may hold values from 0.1 to 1.9
Outputs:
- block_out: bfloat16 [2048, 6144], P(('cuts', 'dp', 'mp'))
- attn_grad: bfloat16 [2048, 3072], P(('cuts', 'dp'), 'mp')
- weight_grad: float32 [3072, 6144], P('mp', 'dp')
All inputs are finite; a program needn't handle non-finite values.
Results may differ from a plain program's by a relative error of at most 0.018.
Values may be sent and summed in bfloat16 or wider, within the bound.
A program may use at most 128 MiB of HBM per device.

v0:
```python
import functools

import jax
import jax.numpy as jnp
from jax import lax
from jax.experimental import pallas as pl
from jax.experimental.pallas import tpu as pltpu
from jax.sharding import PartitionSpec as P

epsilon = 1e-06


def norm_backward(stream, target, norm_gain):
    center = stream - jnp.mean(stream, axis=1, keepdims=True)
    inv_std = lax.rsqrt(jnp.mean(center * center, axis=1, keepdims=True) + epsilon)
    normed = center * inv_std
    misfit = normed * norm_gain[None, :] - target.astype(jnp.float32)
    gain_err = misfit * norm_gain[None, :]
    bracket = (
        gain_err
        - jnp.mean(gain_err, axis=1, keepdims=True)
        - normed * jnp.mean(gain_err * normed, axis=1, keepdims=True)
    )
    return (inv_std * bracket).astype(jnp.bfloat16)


def per_device(attn_out, out_weight, residual, target, norm_gain):
    tokens_dev = attn_out.shape[0]
    head_cols = attn_out.shape[1]
    replica_scale = 1.0 / (lax.axis_size("cuts") * lax.axis_size("dp"))
    summed = lax.psum_scatter(
        jnp.dot(attn_out, out_weight, preferred_element_type=jnp.float32).astype(jnp.bfloat16),
        "mp",
        scatter_dimension=0,
        tiled=True,
    ).astype(jnp.float32)
    stream = summed + residual.astype(jnp.float32)
    block_out = stream.astype(jnp.bfloat16)
    cotangent = norm_backward(stream, target, norm_gain)
    portion = lax.all_gather(cotangent, "mp", axis=0, tiled=True)
    stored = portion
    act_acc = lax.dot_general(
        portion, out_weight, (((1,), (1,)), ((), ())), preferred_element_type=jnp.float32
    )
    collected, act_acc = (stored, act_acc)
    attn_grad = act_acc.astype(jnp.bfloat16)
    columns = lax.all_to_all(collected, "dp", split_axis=1, concat_axis=0, tiled=True)
    column_width = columns.shape[1]
    portion = lax.all_gather(attn_out, "dp", axis=0, tiled=True)
    blocks_in = portion.shape[0] // tokens_dev
    head_block = portion.reshape(blocks_in, tokens_dev, head_cols)
    column_part = columns.reshape(blocks_in, tokens_dev, column_width)
    shares = (
        jnp.einsum("bti,btj->bij", head_block, column_part, preferred_element_type=jnp.float32)
        * replica_scale
    )
    rounded = lax.optimization_barrier(shares.astype(jnp.bfloat16))
    grad_block = jnp.sum(rounded.astype(jnp.float32), axis=0)
    weight_grad = lax.psum(grad_block.astype(jnp.bfloat16), "cuts").astype(jnp.float32)
    return (block_out, attn_grad, weight_grad)


MESH = pl.DeviceIdType.MESH


def remote(src, dst, send_sem, recv_sem, **where):
    return pltpu.make_async_remote_copy(
        src_ref=src, dst_ref=dst, send_sem=send_sem, recv_sem=recv_sem, device_id=where, device_id_type=MESH
    )


def fused(
    nz, ndp, chunk, attn_h, w_h, res_h, tgt_h, gain_h, blk_o, agrad_o, wgrad_o,
    w_v, a_v, rows_v, cot_v, part, part_in, res_v, tgt_v, gain_v, blk_v, agrad_v, acc, out_v,
    ld_s, w_s, p_s, p_r, au_s, ad_s, az_r, ap_s, ap_r, cp_s, cq_s, cq_r, cu_s, cd_s, c_r, ce_s, ce_r, o_s,
):
    z, dp, m = lax.axis_index("cuts"), lax.axis_index("dp"), lax.axis_index("mp")
    other = 1 - m
    tok, heads = attn_h.shape
    half, width = res_h.shape
    cols = width // ndp
    chunks = width // chunk
    has_up, has_down = z + 1 < nz, z >= 1
    scale = 1.0 / (nz * ndp)

    loads = [
        pltpu.make_async_copy(attn_h, a_v.at[z, dp], ld_s.at[0]),
        pltpu.make_async_copy(res_h, res_v, ld_s.at[1]),
        pltpu.make_async_copy(tgt_h, tgt_v, ld_s.at[2]),
        pltpu.make_async_copy(gain_h, gain_v, ld_s.at[3]),
    ]
    loads[0].start()

    def w_load(c):
        at = pl.ds(pl.multiple_of(c * chunk, chunk), chunk)
        return pltpu.make_async_copy(w_h.at[:, at], w_v.at[:, at], w_s.at[c])

    for c in range(chunks):
        w_load(c).start()
    for load in loads[1:]:
        load.start()

    barrier = pltpu.get_barrier_semaphore()
    pl.semaphore_signal(barrier, inc=1, device_id={"mp": other}, device_id_type=MESH)
    for k in range(1, ndp):
        pl.semaphore_signal(barrier, inc=1, device_id={"dp": lax.rem(dp + k, ndp)}, device_id_type=MESH)

    @pl.when(has_up)
    def _():
        pl.semaphore_signal(barrier, inc=1, device_id={"cuts": z + 1}, device_id_type=MESH)

    @pl.when(has_down)
    def _():
        pl.semaphore_signal(barrier, inc=1, device_id={"cuts": z - 1}, device_id_type=MESH)

    pl.semaphore_wait(barrier, ndp + jnp.where(has_up, 1, 0) + jnp.where(has_down, 1, 0))

    def a_up(l):
        return remote(a_v.at[l, dp], a_v.at[l, dp], au_s.at[l], az_r.at[l], cuts=z + 1)

    def a_down(l):
        return remote(a_v.at[l, dp], a_v.at[l, dp], ad_s.at[l], az_r.at[l], cuts=z - 1)

    def a_plane(l, k):
        return remote(a_v.at[l, dp], a_v.at[l, dp], ap_s.at[l, k], ap_r.at[l, dp], dp=lax.rem(dp + k, ndp))

    def a_plane_in(l, k):
        src = lax.rem(dp + ndp - k, ndp)
        return remote(a_v.at[l, src], a_v.at[l, src], ap_s.at[l, k], ap_r.at[l, src], dp=src)

    def c_up(l, d, src=None):
        return remote(cot_v.at[l, d, m] if src is None else src, cot_v.at[l, d, m], cu_s.at[l, d], c_r.at[l, d], cuts=z + 1)

    def c_down(l, d, src=None):
        return remote(cot_v.at[l, d, m] if src is None else src, cot_v.at[l, d, m], cd_s.at[l, d], c_r.at[l, d], cuts=z - 1)

    def c_pair(l, d):
        return remote(cot_v.at[l, d, m], cot_v.at[l, d, m], ce_s.at[l, d], ce_r.at[l, d], mp=other)

    def c_pair_in(l, d):
        return remote(cot_v.at[l, d, other], cot_v.at[l, d, other], ce_s.at[l, d], ce_r.at[l, d], mp=other)

    def a_hop(k):
        low, high = z - k, z + k

        @pl.when(low >= 0)
        def _():
            a_up(low).wait_recv()

            @pl.when(has_up)
            def _():
                a_up(low).start()

        @pl.when(high < nz)
        def _():
            a_down(high).wait_recv()

            @pl.when(has_down)
            def _():
                a_down(high).start()

    def both(k, f):
        pl.when(z - k >= 0)(lambda: f(z - k))
        pl.when(z + k < nz)(lambda: f(z + k))

    loads[0].wait()

    @pl.when(has_up)
    def _():
        a_up(z).start()

    @pl.when(has_down)
    def _():
        a_down(z).start()

    for k in range(1, ndp):
        a_plane(z, k).start()

    def p_send(c):
        at = pl.ds(pl.multiple_of(c * chunk, chunk), chunk)
        return remote(part.at[other, :, at], part_in.at[:, at], p_s.at[c], p_r.at[c], mp=other)

    @pl.loop(0, chunks)
    def _(c):
        at = pl.ds(pl.multiple_of(c * chunk, chunk), chunk)
        w_load(c).wait()
        value = jnp.dot(a_v[z, dp], w_v[:, at], preferred_element_type=jnp.float32).astype(jnp.bfloat16)
        part[0, :, at] = value[:half]
        part[1, :, at] = value[half:]
        p_send(c).start()

    a_hop(1)
    for load in loads[1:]:
        load.wait()

    @pl.loop(0, chunks)
    def _(c):
        p_send(c).wait()

    step = 16
    gain = gain_v[...]

    @pl.loop(0, half // step)
    def _(i):
        at = pl.ds(pl.multiple_of(i * step, step), step)
        stream = (
            part[m, at, :].astype(jnp.float32) + part_in[at, :].astype(jnp.float32) + res_v[at, :].astype(jnp.float32)
        )
        blk_v[at, :] = stream.astype(jnp.bfloat16)
        center = stream - jnp.mean(stream, axis=1, keepdims=True)
        inv_std = lax.rsqrt(jnp.mean(center * center, axis=1, keepdims=True) + epsilon)
        normed = center * inv_std
        gain_err = (normed * gain - tgt_v[at, :].astype(jnp.float32)) * gain
        bracket = (
            gain_err
            - jnp.mean(gain_err, axis=1, keepdims=True)
            - normed * jnp.mean(gain_err * normed, axis=1, keepdims=True)
        )
        cot = (inv_std * bracket).astype(jnp.bfloat16)
        for d in range(ndp):
            rows_v[d, m, at, :] = cot[:, d * cols : (d + 1) * cols]

    def c_plane(k):
        to = lax.rem(dp + k, ndp)
        return remote(rows_v.at[to, m], cot_v.at[z, dp, m], cp_s.at[k], c_r.at[z, dp], dp=to)

    def c_rows():
        return remote(rows_v.at[:, m], rows_v.at[:, m], cq_s.at[0], cq_r.at[0], mp=other)

    def c_rows_in():
        return remote(rows_v.at[:, other], rows_v.at[:, other], cq_s.at[0], cq_r.at[0], mp=other)

    for k in range(1, ndp):
        c_plane(k).start()
    own = rows_v.at[dp, m]

    @pl.when(has_up)
    def _():
        c_up(z, dp, own).start()

    @pl.when(has_down)
    def _():
        c_down(z, dp, own).start()

    c_rows().start()
    blk_copy = pltpu.make_async_copy(blk_v, blk_o, ld_s.at[1])
    blk_copy.start()
    cot_v[z, dp, m] = rows_v[dp, m]

    both(1, lambda l: [a_plane(l, k).start() for k in range(1, ndp)] and None)
    c_rows_in().wait_recv()
    cot_v[z, dp, other] = rows_v[dp, other]

    def c_forward(l, d, up, down):
        pl.when(up)(lambda: c_up(l, d).start())
        pl.when(down)(lambda: c_down(l, d).start())
        c_pair(l, d).start()

    for k in range(1, ndp):
        d = lax.rem(dp + ndp - k, ndp)
        c_up(z, d).wait_recv()
        c_forward(z, d, has_up, has_down)
    for k in range(2, nz):
        a_hop(k)
        both(k, lambda l: [a_plane(l, j).start() for j in range(1, ndp)] and None)

    tile = 512 if heads % 512 == 0 else heads

    @pl.loop(0, heads // tile)
    def _(j):
        at = pl.ds(pl.multiple_of(j * tile, tile), tile)
        total = jnp.zeros((tok, tile), jnp.float32)
        for d in range(ndp):
            total += lax.dot_general(
                rows_v[d].reshape(tok, cols), w_v[at, d * cols : (d + 1) * cols], (((1,), (1,)), ((), ())),
                preferred_element_type=jnp.float32,
            )
        agrad_v[:, at] = total.astype(jnp.bfloat16)

    agrad_copy = pltpu.make_async_copy(agrad_v, agrad_o, ld_s.at[2])
    agrad_copy.start()

    wide = 256 if heads % 256 == 0 else heads

    far = jnp.maximum(z, nz - 1 - z)

    def out_copy(j):
        at = pl.ds(pl.multiple_of(j * wide, wide), wide)
        return pltpu.make_async_copy(out_v.at[at, :], wgrad_o.at[at, :], o_s.at[j])

    def group(l, first, last):
        for k in range(1, ndp):
            a_plane_in(l, k).wait_recv()

        @pl.loop(0, heads // wide)
        def _(j):
            at = pl.ds(pl.multiple_of(j * wide, wide), wide)
            value = scale * lax.dot_general(
                a_v[l, :, :, at].reshape(ndp * tok, wide), cot_v[l].reshape(ndp * tok, cols), (((0,), (0,)), ((), ())),
                preferred_element_type=jnp.float32,
            )
            value = value if first else acc[at, :] + value
            acc[at, :] = value

            @pl.when(last)
            def _():
                out_v[at, :] = value.astype(jnp.bfloat16)
                out_copy(j).start()

    for k in range(1, ndp):
        c_pair_in(z, lax.rem(dp + ndp - k, ndp)).wait_recv()
    group(z, True, far == 0)

    @pl.loop(1, nz)
    def _(k):
        for j in range(ndp):
            d = lax.rem(dp + ndp - j, ndp)

            @pl.when(z - k >= 0)
            def _():
                c_up(z - k, d).wait_recv()
                c_forward(z - k, d, has_up, False)

            @pl.when(z + k < nz)
            def _():
                c_down(z + k, d).wait_recv()
                c_forward(z + k, d, False, has_down)

        def finish(l):
            for j in range(ndp):
                c_pair_in(l, j).wait_recv()
            group(l, False, (l == z + far) | ((l == z - far) & (z + far >= nz)))

        both(k, finish)

    @pl.loop(0, nz)
    def _(l):
        @pl.when(has_up & (l <= z))
        def _():
            a_up(l).wait_send()
            for d in range(ndp):
                c_up(l, d).wait_send()

        @pl.when(has_down & (l >= z))
        def _():
            a_down(l).wait_send()
            for d in range(ndp):
                c_down(l, d).wait_send()

        for k in range(1, ndp):
            a_plane(l, k).wait_send()
            c_pair(l, lax.rem(dp + k, ndp)).wait_send()

        @pl.when(l != z)
        def _():
            c_pair(l, dp).wait_send()

    for k in range(1, ndp):
        c_plane(k).wait_send()
    c_rows().wait_send()
    blk_copy.wait()
    agrad_copy.wait()

    @pl.loop(0, heads // wide)
    def _(j):
        out_copy(j).wait()


def widen(blk_i, agrad_i, wgrad_i, blk_o, agrad_o, wgrad_o):
    blk_o[...] = blk_i[...]
    agrad_o[...] = agrad_i[...]
    wgrad_o[...] = wgrad_i[...].astype(jnp.float32)


def fused_device(nz, ndp, attn_out, out_weight, residual, target, norm_gain):
    tok, heads = attn_out.shape
    half, width = residual.shape
    cols = width // ndp
    chunk = 512 if width % 512 == 0 else 128
    chunks = width // chunk
    tiles = heads // 256 if heads % 256 == 0 else 1
    bf16, f32 = jnp.bfloat16, jnp.float32
    dma = pltpu.SemaphoreType.DMA
    any_space = pl.BlockSpec(memory_space=pl.ANY)
    blk, agrad, wgrad = pl.pallas_call(
        functools.partial(fused, nz, ndp, chunk),
        out_shape=(
            jax.ShapeDtypeStruct((half, width), bf16),
            jax.ShapeDtypeStruct((tok, heads), bf16),
            jax.ShapeDtypeStruct((heads, cols), bf16),
        ),
        in_specs=[any_space] * 5,
        out_specs=(any_space,) * 3,
        scratch_shapes=[
            pltpu.VMEM((heads, width), bf16),
            pltpu.VMEM((nz, ndp, tok, heads), bf16),
            pltpu.VMEM((ndp, 2, half, cols), bf16),
            pltpu.VMEM((nz, ndp, 2, half, cols), bf16),
            pltpu.VMEM((2, half, width), bf16),
            pltpu.VMEM((half, width), bf16),
            pltpu.VMEM((half, width), bf16),
            pltpu.VMEM((half, width), bf16),
            pltpu.VMEM((1, width), f32),
            pltpu.VMEM((half, width), bf16),
            pltpu.VMEM((tok, heads), bf16),
            pltpu.VMEM((heads, cols), f32),
            pltpu.VMEM((heads, cols), bf16),
            dma((4,)), dma((chunks,)), dma((chunks,)), dma((chunks,)),
            dma((nz,)), dma((nz,)), dma((nz,)), dma((nz, ndp)), dma((nz, ndp)),
            dma((ndp,)), dma((1,)), dma((1,)),
            dma((nz, ndp)), dma((nz, ndp)), dma((nz, ndp)), dma((nz, ndp)), dma((nz, ndp)), dma((tiles,)),
        ],
        compiler_params=pltpu.CompilerParams(
            collective_id=0, has_side_effects=True, vmem_limit_bytes=66 * 1000 * 1000
        ),
    )(attn_out, out_weight, residual, target, norm_gain.reshape(1, width))
    parts = tiles if width % (tiles * 128) == 0 and heads % (tiles * 128) == 0 else 1
    specs = [
        pl.BlockSpec((half, width // parts), lambda i: (0, i)),
        pl.BlockSpec((tok, heads // parts), lambda i: (0, i)),
        pl.BlockSpec((heads // parts, cols), lambda i: (i, 0)),
    ]
    return pl.pallas_call(
        widen,
        grid=(parts,),
        out_shape=(
            jax.ShapeDtypeStruct((half, width), bf16),
            jax.ShapeDtypeStruct((tok, heads), bf16),
            jax.ShapeDtypeStruct((heads, cols), f32),
        ),
        in_specs=specs,
        out_specs=tuple(specs),
        compiler_params=pltpu.CompilerParams(vmem_limit_bytes=66 * 1000 * 1000),
    )(blk, agrad, wgrad)


def solution(mesh):
    if mesh.shape["mp"] == 2:
        body = functools.partial(fused_device, mesh.shape["cuts"], mesh.shape["dp"])
    else:
        body = per_device
    placed = (
        P(("cuts", "dp"), "mp"),
        P("mp", None),
        P(("cuts", "dp", "mp"), None),
        P(("cuts", "dp", "mp"), None),
        P(),
    )
    return jax.shard_map(
        body,
        mesh=mesh,
        in_specs=placed,
        out_specs=(P(("cuts", "dp", "mp"), None), P(("cuts", "dp"), "mp"), P("mp", "dp")),
        check_vma=False,
    )
```

profile of v0, /device:TPU:0, one launch (start us, length us, event | category | flops | bytes accessed | tf_op | source)
XLA Modules:
  0.0 104.6 jit_solution(8415336403477857901)
XLA Ops:
  0.6 96.4 %shard_map.76 = (bf16[64,6144]{1,0:T(8,128)(2,1)}, bf16[128,1536]{1,0:T(8,128)(2,1)}, bf16[1536,1536]{1,0:T(8,128)(2,1)}) custom-call(bf16[128,1536]{1,0:T(8,128)(2,1)} %attn_h.1, bf16[1536,6144]{1,0:T(8,128)(2,1)} %w_h.1, bf16[64,6144]{1,0:T(8,128)(2,1)} %res_h.1, bf16[64,6144]{1,0:T(8,128)(2,1)} %tgt_h.1, f32[1,6144]{1,0:T(1,128)} %bitcast.1), custom_call_target="tpu_custom_call" | custom-call | tf_op jit(solution)/shard_map/pallas_call | solution.py:385
  97.0 7.6 %shard_map.77 = (bf16[64,6144]{1,0:T(8,128)(2,1)}, bf16[128,1536]{1,0:T(8,128)(2,1)}, f32[1536,1536]{1,0:T(8,128)}) custom-call(bf16[64,6144]{1,0:T(8,128)(2,1)} %get-tuple-element.6.blk_i, bf16[128,1536]{1,0:T(8,128)(2,1)} %get-tuple-element.7.agrad_i, bf16[1536,1536]{1,0:T(8,128)(2,1)} %get-tuple-element.8.wgrad_i), custom_call_target="tpu_custom_call" | custom-call | tf_op jit(solution)/shard_map/pallas_call | solution.py:423
where the time goes:
time: 106 us; the launch traced here: 105 us
  Pallas kernels  104 us (98%)
    pallas_call x1, Pallas kernels, fused_device(): pl.pallas_call(functools.partial(fused, nz, ndp, chunk), out_shape=(jax.S...  96.4 us
    pallas_call x1, Pallas kernels, fused_device(): pl.pallas_call(widen, grid=(parts,), out_shape=(jax.ShapeDtypeStruct((hal...  7.57 us

commit v1 on v0

v1 whole, which is shorter than its diff:
```python
import functools

import jax
import jax.numpy as jnp
from jax import lax
from jax.experimental import pallas as pl
from jax.experimental.pallas import tpu as pltpu
from jax.sharding import PartitionSpec as P

epsilon = 1e-06


def norm_backward(stream, target, norm_gain):
    center = stream - jnp.mean(stream, axis=1, keepdims=True)
    inv_std = lax.rsqrt(jnp.mean(center * center, axis=1, keepdims=True) + epsilon)
    normed = center * inv_std
    misfit = normed * norm_gain[None, :] - target.astype(jnp.float32)
    gain_err = misfit * norm_gain[None, :]
    bracket = (
        gain_err
        - jnp.mean(gain_err, axis=1, keepdims=True)
        - normed * jnp.mean(gain_err * normed, axis=1, keepdims=True)
    )
    return (inv_std * bracket).astype(jnp.bfloat16)


def per_device(attn_out, out_weight, residual, target, norm_gain):
    tokens_dev = attn_out.shape[0]
    head_cols = attn_out.shape[1]
    replica_scale = 1.0 / (lax.axis_size("cuts") * lax.axis_size("dp"))
    summed = lax.psum_scatter(
        jnp.dot(attn_out, out_weight, preferred_element_type=jnp.float32).astype(jnp.bfloat16),
        "mp",
        scatter_dimension=0,
        tiled=True,
    ).astype(jnp.float32)
    stream = summed + residual.astype(jnp.float32)
    block_out = stream.astype(jnp.bfloat16)
    cotangent = norm_backward(stream, target, norm_gain)
    portion = lax.all_gather(cotangent, "mp", axis=0, tiled=True)
    stored = portion
    act_acc = lax.dot_general(
        portion, out_weight, (((1,), (1,)), ((), ())), preferred_element_type=jnp.float32
    )
    collected, act_acc = (stored, act_acc)
    attn_grad = act_acc.astype(jnp.bfloat16)
    columns = lax.all_to_all(collected, "dp", split_axis=1, concat_axis=0, tiled=True)
    column_width = columns.shape[1]
    portion = lax.all_gather(attn_out, "dp", axis=0, tiled=True)
    blocks_in = portion.shape[0] // tokens_dev
    head_block = portion.reshape(blocks_in, tokens_dev, head_cols)
    column_part = columns.reshape(blocks_in, tokens_dev, column_width)
    shares = (
        jnp.einsum("bti,btj->bij", head_block, column_part, preferred_element_type=jnp.float32)
        * replica_scale
    )
    rounded = lax.optimization_barrier(shares.astype(jnp.bfloat16))
    grad_block = jnp.sum(rounded.astype(jnp.float32), axis=0)
    weight_grad = lax.psum(grad_block.astype(jnp.bfloat16), "cuts").astype(jnp.float32)
    return (block_out, attn_grad, weight_grad)


NS = jax.named_scope
MESH = pl.DeviceIdType.MESH


def remote(src, dst, send_sem, recv_sem, **where):
    return pltpu.make_async_remote_copy(
        src_ref=src, dst_ref=dst, send_sem=send_sem, recv_sem=recv_sem, device_id=where, device_id_type=MESH
    )


def last_plane(nz, z):
    return jnp.where(2 * z < nz - 1, nz - 1, 0)


def fused(
    nz, ndp, chunk, attn_h, w_h, res_h, tgt_h, gain_h, blk_v, agrad_v, acc, a_v, cot_v,
    w_v, rows_v, part, part_in, res_v, tgt_v, gain_v,
    ld_s, w_s, p_s, p_r, au_s, ad_s, az_r, ax_s, ax_r, ay_s, ay_r, rx_s, rx_r, ry_s, ry_r,
    cp_s, cq_s, cq_r, cu_s, cd_s, c_r, ce_s, ce_r,
):
    z, dp, m = lax.axis_index("cuts"), lax.axis_index("dp"), lax.axis_index("mp")
    other = 1 - m
    px, py = lax.rem(dp, 2), lax.div(dp, 2)
    xn, yn, dg = 2 * py + 1 - px, 2 * (1 - py) + px, 2 * (1 - py) + 1 - px
    peers = (dp, xn, yn, dg)
    tok, heads = attn_h.shape
    half, width = res_h.shape
    cols = width // ndp
    chunks = width // chunk
    has_up, has_down = z + 1 < nz, z >= 1

    a_load = pltpu.make_async_copy(attn_h, a_v.at[z, dp], ld_s.at[0])
    loads = [
        pltpu.make_async_copy(res_h, res_v, ld_s.at[1]),
        pltpu.make_async_copy(tgt_h, tgt_v, ld_s.at[2]),
        pltpu.make_async_copy(gain_h, gain_v, ld_s.at[3]),
    ]
    a_load.start()

    def w_load(c):
        at = pl.ds(pl.multiple_of(c * chunk, chunk), chunk)
        return pltpu.make_async_copy(w_h.at[:, at], w_v.at[:, at], w_s.at[c])

    barrier = pltpu.get_barrier_semaphore()
    pl.semaphore_signal(barrier, inc=1, device_id={"mp": other}, device_id_type=MESH)
    for peer in peers[1:]:
        pl.semaphore_signal(barrier, inc=1, device_id={"dp": peer}, device_id_type=MESH)

    @pl.when(has_up)
    def _():
        pl.semaphore_signal(barrier, inc=1, device_id={"cuts": z + 1}, device_id_type=MESH)

    @pl.when(has_down)
    def _():
        pl.semaphore_signal(barrier, inc=1, device_id={"cuts": z - 1}, device_id_type=MESH)

    with NS("aload"):
        a_load.wait()
    for c in range(chunks):
        w_load(c).start()
    for load in loads:
        load.start()
    with NS("barrier"):
        pl.semaphore_wait(barrier, ndp + jnp.where(has_up, 1, 0) + jnp.where(has_down, 1, 0))

    def rows(h):
        return pl.ds(h * half, half)

    def piece(l, d, h):
        return a_v.at[l, d, rows(h)]

    def a_up(l, h):
        return remote(piece(l, dp, h), piece(l, dp, h), au_s.at[l, h], az_r.at[l, h], cuts=z + 1)

    def a_down(l, h):
        return remote(piece(l, dp, h), piece(l, dp, h), ad_s.at[l, h], az_r.at[l, h], cuts=z - 1)

    def a_x(l, h):
        return remote(piece(l, dp, h), piece(l, dp, h), ax_s.at[l, h], ax_r.at[l, h], dp=xn)

    def a_y(l, h):
        return remote(piece(l, dp, h), piece(l, dp, h), ay_s.at[l, h], ay_r.at[l, h], dp=yn)

    def a_x_in(l, h):
        return remote(piece(l, xn, h), piece(l, xn, h), ax_s.at[l, h], ax_r.at[l, h], dp=xn)

    def a_y_in(l, h):
        return remote(piece(l, yn, h), piece(l, yn, h), ay_s.at[l, h], ay_r.at[l, h], dp=yn)

    def r_y(l):
        return remote(piece(l, xn, 0), piece(l, xn, 0), ry_s.at[l], ry_r.at[l], dp=yn)

    def r_x(l):
        return remote(piece(l, yn, 1), piece(l, yn, 1), rx_s.at[l], rx_r.at[l], dp=xn)

    def r_y_in(l):
        return remote(piece(l, dg, 0), piece(l, dg, 0), ry_s.at[l], ry_r.at[l], dp=yn)

    def r_x_in(l):
        return remote(piece(l, dg, 1), piece(l, dg, 1), rx_s.at[l], rx_r.at[l], dp=xn)

    def c_up(l, d, src=None):
        return remote(cot_v.at[l, d, m] if src is None else src, cot_v.at[l, d, m], cu_s.at[l, d], c_r.at[l, d], cuts=z + 1)

    def c_down(l, d, src=None):
        return remote(cot_v.at[l, d, m] if src is None else src, cot_v.at[l, d, m], cd_s.at[l, d], c_r.at[l, d], cuts=z - 1)

    def c_pair(l, d):
        return remote(cot_v.at[l, d, m], cot_v.at[l, d, m], ce_s.at[l, d], ce_r.at[l, d], mp=other)

    def c_pair_in(l, d):
        return remote(cot_v.at[l, d, other], cot_v.at[l, d, other], ce_s.at[l, d], ce_r.at[l, d], mp=other)

    def both(k, f):
        pl.when(z - k >= 0)(lambda: f(z - k))
        pl.when(z + k < nz)(lambda: f(z + k))

    def a_hop(k, h):
        if k >= nz:
            return

        @pl.when(z - k >= 0)
        def _():
            with NS("ahop"):
                a_up(z - k, h).wait_recv()
            pl.when(has_up)(lambda: a_up(z - k, h).start())

        @pl.when(z + k < nz)
        def _():
            with NS("ahop"):
                a_down(z + k, h).wait_recv()
            pl.when(has_down)(lambda: a_down(z + k, h).start())

    def a_plane(l):
        a_x(l, 0).start()
        a_y(l, 1).start()
        a_x(l, 1).start()
        a_y(l, 0).start()

    def relay(l):
        with NS("relay"):
            a_x_in(l, 0).wait_recv()
        r_y(l).start()
        with NS("relay"):
            a_y_in(l, 1).wait_recv()
        r_x(l).start()

    for h in range(2):
        pl.when(has_up)(lambda: a_up(z, h).start())
        pl.when(has_down)(lambda: a_down(z, h).start())
    a_plane(z)

    def p_send(c):
        at = pl.ds(pl.multiple_of(c * chunk, chunk), chunk)
        return remote(part.at[other, :, at], part_in.at[:, at], p_s.at[c], p_r.at[c], mp=other)

    @pl.loop(0, chunks)
    def _(c):
        at = pl.ds(pl.multiple_of(c * chunk, chunk), chunk)
        with NS("wload"):
            w_load(c).wait()
        value = jnp.dot(a_v[z, dp], w_v[:, at], preferred_element_type=jnp.float32).astype(jnp.bfloat16)
        part[0, :, at] = value[:half]
        part[1, :, at] = value[half:]
        p_send(c).start()

    a_hop(1, 0)
    relay(z)
    with NS("loads"):
        for load in loads:
            load.wait()

    with NS("psend"):

        @pl.loop(0, chunks)
        def _(c):
            p_send(c).wait()

    step = 16
    gain = gain_v[...]

    @pl.loop(0, half // step)
    def _(i):
        at = pl.ds(pl.multiple_of(i * step, step), step)
        stream = (
            part[m, at, :].astype(jnp.float32) + part_in[at, :].astype(jnp.float32) + res_v[at, :].astype(jnp.float32)
        )
        blk_v[at, :] = stream.astype(jnp.bfloat16)
        center = stream - jnp.mean(stream, axis=1, keepdims=True)
        inv_std = lax.rsqrt(jnp.mean(center * center, axis=1, keepdims=True) + epsilon)
        normed = center * inv_std
        gain_err = (normed * gain - tgt_v[at, :].astype(jnp.float32)) * gain
        bracket = (
            gain_err
            - jnp.mean(gain_err, axis=1, keepdims=True)
            - normed * jnp.mean(gain_err * normed, axis=1, keepdims=True)
        )
        cot = (inv_std * bracket).astype(jnp.bfloat16)
        for d in range(ndp):
            rows_v[d, m, at, :] = cot[:, d * cols : (d + 1) * cols]

    def c_plane(k):
        return remote(rows_v.at[peers[k], m], cot_v.at[z, dp, m], cp_s.at[k], c_r.at[z, dp], dp=peers[k])

    def c_rows():
        return remote(rows_v.at[:, m], rows_v.at[:, m], cq_s.at[0], cq_r.at[0], mp=other)

    def c_rows_in():
        return remote(rows_v.at[:, other], rows_v.at[:, other], cq_s.at[0], cq_r.at[0], mp=other)

    own = rows_v.at[dp, m]
    pl.when(has_up)(lambda: c_up(z, dp, own).start())
    pl.when(has_down)(lambda: c_down(z, dp, own).start())
    for k in range(1, ndp):
        c_plane(k).start()
    c_rows().start()
    cot_v[z, dp, m] = rows_v[dp, m]

    a_hop(1, 1)
    both(1, a_plane)
    with NS("crows"):
        c_rows_in().wait_recv()
    cot_v[z, dp, other] = rows_v[dp, other]

    tile = 512 if heads % 512 == 0 else heads

    def attn_tile(j):
        at = slice(j * tile, (j + 1) * tile)
        total = jnp.zeros((tok, tile), jnp.float32)
        for d in range(ndp):
            total += lax.dot_general(
                rows_v[d].reshape(tok, cols), w_v[at, d * cols : (d + 1) * cols], (((1,), (1,)), ((), ())),
                preferred_element_type=jnp.float32,
            )
        agrad_v[:, at] = total.astype(jnp.bfloat16)

    def c_forward(l, d, up, down):
        pl.when(up)(lambda: c_up(l, d).start())
        pl.when(down)(lambda: c_down(l, d).start())
        c_pair(l, d).start()

    tiles = heads // tile
    for j in range(tiles):
        attn_tile(j)
        if j < 2:
            a_hop(2, j)
    for h in range(tiles, 2):
        a_hop(2, h)
    both(2, a_plane)
    for k in range(1, ndp):
        with NS("cplane"):
            c_up(z, peers[k]).wait_recv()
        c_forward(z, peers[k], has_up, has_down)

    wide = 256 if heads % 256 == 0 else heads

    def accumulate(l, first, count, fresh):
        @pl.loop(0, heads // wide)
        def _(j):
            at = pl.ds(pl.multiple_of(j * wide, wide), wide)
            value = lax.dot_general(
                a_v[l, pl.ds(first, count), :, at].reshape(count * tok, wide),
                cot_v[l, pl.ds(first, count)].reshape(count * tok, cols),
                (((0,), (0,)), ((), ())),
                preferred_element_type=jnp.float32,
            )
            acc[at, :] = value if fresh else acc[at, :] + value

    def a_arrived(l):
        a_x_in(l, 1).wait_recv()
        a_y_in(l, 0).wait_recv()
        r_y_in(l).wait_recv()
        r_x_in(l).wait_recv()

    with NS("cpair0"):
        for k in range(1, ndp):
            c_pair_in(z, peers[k]).wait_recv()
    with NS("aarr0"):
        a_arrived(z)
    with NS("group0"):
        accumulate(z, 0, ndp, True)

    both(1, relay)
    last = last_plane(nz, z)
    for k in range(1, nz):
        for h in range(2):
            a_hop(k + 2, h)
        if k + 2 < nz:
            both(k + 2, a_plane)
        for j in range(ndp):

            @pl.when(z - k >= 0)
            def _():
                with NS("cup"):
                    c_up(z - k, peers[j]).wait_recv()
                c_forward(z - k, peers[j], has_up, False)

            @pl.when(z + k < nz)
            def _():
                with NS("cdown"):
                    c_down(z + k, peers[j]).wait_recv()
                c_forward(z + k, peers[j], False, has_down)

            if j == 1 and k + 1 < nz:
                both(k + 1, relay)

            def near(l):
                for i in range(2):
                    c_pair_in(l, peers[i]).wait_recv()
                a_x_in(l, 1).wait_recv()
                accumulate(l, 2 * py, 2, False)

            if j == 2:
                both(k, lambda l: pl.when(l == last)(lambda: near(l)))

        def finish(l):
            with NS("cpair"):

                @pl.when(l == last)
                def _():
                    for j in range(2, ndp):
                        c_pair_in(l, peers[j]).wait_recv()
                    a_y_in(l, 0).wait_recv()
                    r_y_in(l).wait_recv()
                    r_x_in(l).wait_recv()

                @pl.when(l != last)
                def _():
                    for j in range(ndp):
                        c_pair_in(l, peers[j]).wait_recv()
                    a_arrived(l)

            @pl.when(l != last)
            def _():
                with NS("group"):
                    accumulate(l, 0, ndp, False)

        both(k, finish)

    @pl.loop(0, nz)
    def _(l):
        @pl.when(has_up & (l <= z))
        def _():
            for h in range(2):
                a_up(l, h).wait_send()
            for d in range(ndp):
                c_up(l, d).wait_send()

        @pl.when(has_down & (l >= z))
        def _():
            for h in range(2):
                a_down(l, h).wait_send()
            for d in range(ndp):
                c_down(l, d).wait_send()

        for h in range(2):
            a_x(l, h).wait_send()
            a_y(l, h).wait_send()
        r_x(l).wait_send()
        r_y(l).wait_send()
        for k in range(1, ndp):
            c_pair(l, peers[k]).wait_send()

        @pl.when(l != z)
        def _():
            c_pair(l, dp).wait_send()

    for k in range(1, ndp):
        c_plane(k).wait_send()
    c_rows().wait_send()


def finishing(nz, ndp, blk_i, agrad_i, acc, a_v, cot_v, blk_o, agrad_o, wgrad_o, out_v, s, o_s):
    z, dp = lax.axis_index("cuts"), lax.axis_index("dp")
    last = last_plane(nz, z)
    first = 2 * (1 - lax.div(dp, 2))
    tok, heads = agrad_i.shape
    cols = acc.shape[1]
    scale = 1.0 / (nz * ndp)
    blk_copy = pltpu.make_async_copy(blk_i, blk_o, s.at[0])
    agrad_copy = pltpu.make_async_copy(agrad_i, agrad_o, s.at[1])
    blk_copy.start()
    agrad_copy.start()
    wide = 256 if heads % 256 == 0 else heads

    def out_copy(j):
        at = pl.ds(pl.multiple_of(j * wide, wide), wide)
        return pltpu.make_async_copy(out_v.at[at, :], wgrad_o.at[at, :], o_s.at[j])

    @pl.loop(0, heads // wide)
    def _(j):
        at = pl.ds(pl.multiple_of(j * wide, wide), wide)
        value = lax.dot_general(
            a_v[last, pl.ds(first, 2), :, at].reshape(2 * tok, wide),
            cot_v[last, pl.ds(first, 2)].reshape(2 * tok, cols),
            (((0,), (0,)), ((), ())),
            preferred_element_type=jnp.float32,
        )
        out_v[at, :] = scale * (acc[at, :] + value)
        out_copy(j).start()

    blk_copy.wait()
    agrad_copy.wait()

    @pl.loop(0, heads // wide)
    def _(j):
        out_copy(j).wait()


def fused_device(nz, ndp, attn_out, out_weight, residual, target, norm_gain):
    tok, heads = attn_out.shape
    half, width = residual.shape
    cols = width // ndp
    chunk = 512 if width % 512 == 0 else 128
    chunks = width // chunk
    tiles = heads // 256 if heads % 256 == 0 else 1
    bf16, f32 = jnp.bfloat16, jnp.float32
    dma = pltpu.SemaphoreType.DMA
    in_vmem = pl.BlockSpec(memory_space=pltpu.VMEM)
    in_hbm = pl.BlockSpec(memory_space=pl.ANY)
    args = [attn_out, out_weight, residual, target, norm_gain.reshape(1, width)]
    args = [pltpu.with_memory_space_constraint(arg, pltpu.HBM) for arg in args]
    kept = pl.pallas_call(
        functools.partial(fused, nz, ndp, chunk),
        out_shape=(
            pltpu.VMEM((half, width), bf16),
            pltpu.VMEM((tok, heads), bf16),
            pltpu.VMEM((heads, cols), f32),
            pltpu.VMEM((nz, ndp, tok, heads), bf16),
            pltpu.VMEM((nz, ndp, 2, half, cols), bf16),
        ),
        in_specs=[in_hbm] * 5,
        out_specs=(in_vmem,) * 5,
        scratch_shapes=[
            pltpu.VMEM((heads, width), bf16),
            pltpu.VMEM((ndp, 2, half, cols), bf16),
            pltpu.VMEM((2, half, width), bf16),
            pltpu.VMEM((half, width), bf16),
            pltpu.VMEM((half, width), bf16),
            pltpu.VMEM((half, width), bf16),
            pltpu.VMEM((1, width), f32),
            dma((4,)), dma((chunks,)), dma((chunks,)), dma((chunks,)),
            dma((nz, 2)), dma((nz, 2)), dma((nz, 2)),
            dma((nz, 2)), dma((nz, 2)), dma((nz, 2)), dma((nz, 2)),
            dma((nz,)), dma((nz,)), dma((nz,)), dma((nz,)),
            dma((ndp,)), dma((1,)), dma((1,)),
            dma((nz, ndp)), dma((nz, ndp)), dma((nz, ndp)), dma((nz, ndp)), dma((nz, ndp)),
        ],
        compiler_params=pltpu.CompilerParams(
            collective_id=0, has_side_effects=True, vmem_limit_bytes=34 * 1000 * 1000
        ),
    )(*args)
    return pl.pallas_call(
        functools.partial(finishing, nz, ndp),
        out_shape=(
            jax.ShapeDtypeStruct((half, width), bf16),
            jax.ShapeDtypeStruct((tok, heads), bf16),
            jax.ShapeDtypeStruct((heads, cols), f32),
        ),
        in_specs=[in_vmem] * 5,
        out_specs=(in_hbm,) * 3,
        scratch_shapes=[pltpu.VMEM((heads, cols), f32), dma((2,)), dma((tiles,))],
        compiler_params=pltpu.CompilerParams(vmem_limit_bytes=16 * 1000 * 1000),
    )(*kept)


def solution(mesh):
    if mesh.shape["mp"] == 2 and mesh.shape["dp"] == 4 and mesh.shape["cuts"] > 1:
        body = functools.partial(fused_device, mesh.shape["cuts"], mesh.shape["dp"])
    else:
        body = per_device
    placed = (
        P(("cuts", "dp"), "mp"),
        P("mp", None),
        P(("cuts", "dp", "mp"), None),
        P(("cuts", "dp", "mp"), None),
        P(),
    )
    return jax.shard_map(
        body,
        mesh=mesh,
        in_specs=placed,
        out_specs=(P(("cuts", "dp", "mp"), None), P(("cuts", "dp"), "mp"), P("mp", "dp")),
        check_vma=False,
    )
```

time: 106 us -> 89.9 us (0.85); the launches traced: 105 us -> 89.7 us
  Pallas kernels: 104 us -> 89 us
    pallas_call x2, Pallas kernels: 104 us -> 89 us  [the longest x1 84.9 us: fused_device(): pl.pallas_call(functools.partial(fused, nz, ndp, chunk), out_shape=(pltpu...]
where the time goes in v1:
time: 89.9 us; the launch traced here: 89.7 us
  Pallas kernels  89 us (99%)
    pallas_call x1, Pallas kernels, fused_device(): pl.pallas_call(functools.partial(fused, nz, ndp, chunk), out_shape=(pltpu...  84.9 us
    pallas_call x1, Pallas kernels, fused_device(): pl.pallas_call(functools.partial(finishing, nz, ndp), out_shape=(jax.Shap...  4.08 us

profile of v1, /device:TPU:0, one launch (start us, length us, event | category | flops | bytes accessed | tf_op | source)
XLA Modules:
  0.0 89.7 jit_solution(12397316423937526213)
XLA Ops:
  0.6 84.9 %shard_map.76 = (bf16[64,6144]{1,0:T(8,128)(2,1)S(1)}, bf16[128,1536]{1,0:T(8,128)(2,1)S(1)}, f32[1536,1536]{1,0:T(8,128)S(1)}, bf16[4,4,128,1536]{3,2,1,0:T(8,128)(2,1)S(1)}, bf16[4,4,2,64,1536]{4,3,2,1,0:T(8,128)(2,1)S(1)}) custom-call(bf16[128,1536]{1,0:T(8,128)(2,1)} %attn_h.1, bf16[1536,6144]{1,0:T(8,128)(2,1)} %w_h.1, bf16[64,6144]{1,0:T(8,128)(2,1)} %res_h.1, ...), custom_call_target="tpu_custom_call" | custom-call | tf_op jit(solution)/shard_map/pallas_call | solution.py:485
  85.6 4.1 %shard_map.77 = (bf16[64,6144]{1,0:T(8,128)(2,1)}, bf16[128,1536]{1,0:T(8,128)(2,1)}, f32[1536,1536]{1,0:T(8,128)}) custom-call(bf16[64,6144]{1,0:T(8,128)(2,1)S(1)} %get-tuple-element.8.blk_i, bf16[128,1536]{1,0:T(8,128)(2,1)S(1)} %get-tuple-element.9.agrad_i, f32[1536,1536]{1,0:T(8,128)S(1)} %get-tuple-element.10.acc, ...), custom_call_target="tpu_custom_call" | custom-call | tf_op jit(solution)/shard_map/pallas_call | solution.py:515

commit v2 on v1

--- a/solution.py
+++ b/solution.py
@@ -77,8 +77,7 @@
 def fused(
     nz, ndp, chunk, attn_h, w_h, res_h, tgt_h, gain_h, blk_v, agrad_v, acc, a_v, cot_v,
     w_v, rows_v, part, part_in, res_v, tgt_v, gain_v,
-    ld_s, w_s, p_s, p_r, au_s, ad_s, az_r, ax_s, ax_r, ay_s, ay_r, rx_s, rx_r, ry_s, ry_r,
-    cp_s, cq_s, cq_r, cu_s, cd_s, c_r, ce_s, ce_r,
+    ld_s, w_s, p_s, p_r, up_s, dn_s, az_r, pl_s, fx_r, fy_r, pl_r, cp_s, cq_s, cq_r, c_r, ce_s, ce_r,
 ):
     z, dp, m = lax.axis_index("cuts"), lax.axis_index("dp"), lax.axis_index("mp")
     other = 1 - m
@@ -89,18 +88,20 @@
     half, width = res_h.shape
     cols = width // ndp
     chunks = width // chunk
+    per_load = 2 if chunks % 2 == 0 else 1
+    last = last_plane(nz, z)
     has_up, has_down = z + 1 < nz, z >= 1
 
     a_load = pltpu.make_async_copy(attn_h, a_v.at[z, dp], ld_s.at[0])
     loads = [
         pltpu.make_async_copy(res_h, res_v, ld_s.at[1]),
-        pltpu.make_async_copy(tgt_h, tgt_v, ld_s.at[2]),
-        pltpu.make_async_copy(gain_h, gain_v, ld_s.at[3]),
+        pltpu.make_async_copy(tgt_h, tgt_v, ld_s.at[1]),
+        pltpu.make_async_copy(gain_h, gain_v, ld_s.at[2]),
     ]
     a_load.start()
 
     def w_load(c):
-        at = pl.ds(pl.multiple_of(c * chunk, chunk), chunk)
+        at = pl.ds(pl.multiple_of(c * per_load * chunk, chunk), per_load * chunk)
         return pltpu.make_async_copy(w_h.at[:, at], w_v.at[:, at], w_s.at[c])
 
     barrier = pltpu.get_barrier_semaphore()
@@ -118,7 +119,7 @@
 
     with NS("aload"):
         a_load.wait()
-    for c in range(chunks):
+    for c in range(chunks // per_load):
         w_load(c).start()
     for load in loads:
         load.start()
@@ -132,46 +133,53 @@
         return a_v.at[l, d, rows(h)]
 
     def a_up(l, h):
-        return remote(piece(l, dp, h), piece(l, dp, h), au_s.at[l, h], az_r.at[l, h], cuts=z + 1)
+        return remote(piece(l, dp, h), piece(l, dp, h), up_s.at[l], az_r.at[l, h], cuts=z + 1)
 
     def a_down(l, h):
-        return remote(piece(l, dp, h), piece(l, dp, h), ad_s.at[l, h], az_r.at[l, h], cuts=z - 1)
+        return remote(piece(l, dp, h), piece(l, dp, h), dn_s.at[l], az_r.at[l, h], cuts=z - 1)
 
     def a_x(l, h):
-        return remote(piece(l, dp, h), piece(l, dp, h), ax_s.at[l, h], ax_r.at[l, h], dp=xn)
+        return remote(piece(l, dp, h), piece(l, dp, h), pl_s.at[l], (fx_r if h == 0 else pl_r).at[l], dp=xn)
 
     def a_y(l, h):
-        return remote(piece(l, dp, h), piece(l, dp, h), ay_s.at[l, h], ay_r.at[l, h], dp=yn)
-
-    def a_x_in(l, h):
-        return remote(piece(l, xn, h), piece(l, xn, h), ax_s.at[l, h], ax_r.at[l, h], dp=xn)
-
-    def a_y_in(l, h):
-        return remote(piece(l, yn, h), piece(l, yn, h), ay_s.at[l, h], ay_r.at[l, h], dp=yn)
+        return remote(piece(l, dp, h), piece(l, dp, h), pl_s.at[l], (fy_r if h == 1 else pl_r).at[l], dp=yn)
+
+    def first_x_in(l):
+        return remote(piece(l, xn, 0), piece(l, xn, 0), pl_s.at[l], fx_r.at[l], dp=xn)
+
+    def first_y_in(l):
+        return remote(piece(l, yn, 1), piece(l, yn, 1), pl_s.at[l], fy_r.at[l], dp=yn)
 
     def r_y(l):
-        return remote(piece(l, xn, 0), piece(l, xn, 0), ry_s.at[l], ry_r.at[l], dp=yn)
+        return remote(piece(l, xn, 0), piece(l, xn, 0), pl_s.at[l], pl_r.at[l], dp=yn)
 
     def r_x(l):
-        return remote(piece(l, yn, 1), piece(l, yn, 1), rx_s.at[l], rx_r.at[l], dp=xn)
-
-    def r_y_in(l):
-        return remote(piece(l, dg, 0), piece(l, dg, 0), ry_s.at[l], ry_r.at[l], dp=yn)
-
-    def r_x_in(l):
-        return remote(piece(l, dg, 1), piece(l, dg, 1), rx_s.at[l], rx_r.at[l], dp=xn)
+        return remote(piece(l, yn, 1), piece(l, yn, 1), pl_s.at[l], pl_r.at[l], dp=xn)
+
+    def rest_in(l):
+        return remote(a_v.at[l, :2], a_v.at[l, :2], pl_s.at[l], pl_r.at[l], dp=xn)
+
+    def sent_up(l):
+        return remote(a_v.at[l, :3], a_v.at[l, :3], up_s.at[l], pl_r.at[l], cuts=z + 1)
+
+    def sent_down(l):
+        return remote(a_v.at[l, :3], a_v.at[l, :3], dn_s.at[l], pl_r.at[l], cuts=z - 1)
+
+    def sent_plane(l):
+        return remote(a_v.at[l, :3], a_v.at[l, :3], pl_s.at[l], pl_r.at[l], dp=xn)
 
     def c_up(l, d, src=None):
-        return remote(cot_v.at[l, d, m] if src is None else src, cot_v.at[l, d, m], cu_s.at[l, d], c_r.at[l, d], cuts=z + 1)
+        return remote(cot_v.at[l, d, m] if src is None else src, cot_v.at[l, d, m], up_s.at[l], c_r.at[l, d], cuts=z + 1)
 
     def c_down(l, d, src=None):
-        return remote(cot_v.at[l, d, m] if src is None else src, cot_v.at[l, d, m], cd_s.at[l, d], c_r.at[l, d], cuts=z - 1)
-
-    def c_pair(l, d):
-        return remote(cot_v.at[l, d, m], cot_v.at[l, d, m], ce_s.at[l, d], ce_r.at[l, d], mp=other)
-
-    def c_pair_in(l, d):
-        return remote(cot_v.at[l, d, other], cot_v.at[l, d, other], ce_s.at[l, d], ce_r.at[l, d], mp=other)
+        return remote(cot_v.at[l, d, m] if src is None else src, cot_v.at[l, d, m], dn_s.at[l], c_r.at[l, d], cuts=z - 1)
+
+    def c_pair(l, d, group):
+        return remote(cot_v.at[l, d, m], cot_v.at[l, d, m], ce_s.at[l], ce_r.at[group], mp=other)
+
+    def c_pairs(l, count, group):
+        blocks = cot_v.at[l, :count, other]
+        return remote(blocks, blocks, ce_s.at[l], ce_r.at[group], mp=other)
 
     def both(k, f):
         pl.when(z - k >= 0)(lambda: f(z - k))
@@ -201,10 +209,10 @@
 
     def relay(l):
         with NS("relay"):
-            a_x_in(l, 0).wait_recv()
+            first_x_in(l).wait_recv()
         r_y(l).start()
         with NS("relay"):
-            a_y_in(l, 1).wait_recv()
+            first_y_in(l).wait_recv()
         r_x(l).start()
 
     for h in range(2):
@@ -214,13 +222,12 @@
 
     def p_send(c):
         at = pl.ds(pl.multiple_of(c * chunk, chunk), chunk)
-        return remote(part.at[other, :, at], part_in.at[:, at], p_s.at[c], p_r.at[c], mp=other)
+        return remote(part.at[other, :, at], part_in.at[:, at], p_s.at[0], p_r.at[0], mp=other)
 
     @pl.loop(0, chunks)
     def _(c):
         at = pl.ds(pl.multiple_of(c * chunk, chunk), chunk)
-        with NS("wload"):
-            w_load(c).wait()
+        pl.when(lax.rem(c, per_load) == 0)(lambda: w_load(lax.div(c, per_load)).wait())
         value = jnp.dot(a_v[z, dp], w_v[:, at], preferred_element_type=jnp.float32).astype(jnp.bfloat16)
         part[0, :, at] = value[:half]
         part[1, :, at] = value[half:]
@@ -229,14 +236,11 @@
     a_hop(1, 0)
     relay(z)
     with NS("loads"):
-        for load in loads:
-            load.wait()
+        pltpu.make_async_copy(part, part, ld_s.at[1]).wait()
+        loads[2].wait()
 
     with NS("psend"):
-
-        @pl.loop(0, chunks)
-        def _(c):
-            p_send(c).wait()
+        remote(part_in, part_in, p_s.at[0], p_r.at[0], mp=other).wait()
 
     step = 16
     gain = gain_v[...]
@@ -262,7 +266,7 @@
             rows_v[d, m, at, :] = cot[:, d * cols : (d + 1) * cols]
 
     def c_plane(k):
-        return remote(rows_v.at[peers[k], m], cot_v.at[z, dp, m], cp_s.at[k], c_r.at[z, dp], dp=peers[k])
+        return remote(rows_v.at[peers[k], m], cot_v.at[z, dp, m], cp_s.at[0], c_r.at[z, dp], dp=peers[k])
 
     def c_rows():
         return remote(rows_v.at[:, m], rows_v.at[:, m], cq_s.at[0], cq_r.at[0], mp=other)
@@ -296,10 +300,10 @@
             )
         agrad_v[:, at] = total.astype(jnp.bfloat16)
 
-    def c_forward(l, d, up, down):
-        pl.when(up)(lambda: c_up(l, d).start())
-        pl.when(down)(lambda: c_down(l, d).start())
-        c_pair(l, d).start()
+    def c_forward(l, j, up, down):
+        pl.when(up)(lambda: c_up(l, peers[j]).start())
+        pl.when(down)(lambda: c_down(l, peers[j]).start())
+        c_pair(l, peers[j], l if j < 2 else jnp.where(l == last, nz, l)).start()
 
     tiles = heads // tile
     for j in range(tiles):
@@ -312,7 +316,7 @@
     for k in range(1, ndp):
         with NS("cplane"):
             c_up(z, peers[k]).wait_recv()
-        c_forward(z, peers[k], has_up, has_down)
+        c_forward(z, k, has_up, has_down)
 
     wide = 256 if heads % 256 == 0 else heads
 
@@ -328,23 +332,34 @@
             )
             acc[at, :] = value if fresh else acc[at, :] + value
 
-    def a_arrived(l):
-        a_x_in(l, 1).wait_recv()
-        a_y_in(l, 0).wait_recv()
-        r_y_in(l).wait_recv()
-        r_x_in(l).wait_recv()
-
     with NS("cpair0"):
-        for k in range(1, ndp):
-            c_pair_in(z, peers[k]).wait_recv()
+        c_pairs(z, ndp - 1, z).wait_recv()
     with NS("aarr0"):
-        a_arrived(z)
+        rest_in(z).wait_recv()
     with NS("group0"):
         accumulate(z, 0, ndp, True)
 
+    def drain():
+        @pl.loop(0, nz)
+        def _(l):
+            pl.when(has_up & (l <= z))(lambda: sent_up(l).wait_send())
+            pl.when(has_down & (l >= z))(lambda: sent_down(l).wait_send())
+            sent_plane(l).wait_send()
+
+            @pl.when((l != last) & (l != z))
+            def _():
+                c_pairs(l, ndp, l).wait_send()
+
+        c_pairs(z, ndp - 1, z).wait_send()
+        blocks = cot_v.at[z, : ndp - 1, m]
+        remote(blocks, blocks, cp_s.at[0], c_r.at[z, dp], dp=xn).wait_send()
+        c_rows().wait_send()
+
     both(1, relay)
-    last = last_plane(nz, z)
     for k in range(1, nz):
+        if k == nz - 1:
+            with NS("drain"):
+                drain()
         for h in range(2):
             a_hop(k + 2, h)
         if k + 2 < nz:
@@ -355,24 +370,24 @@
             def _():
                 with NS("cup"):
                     c_up(z - k, peers[j]).wait_recv()
-                c_forward(z - k, peers[j], has_up, False)
+                c_forward(z - k, j, has_up, False)
 
             @pl.when(z + k < nz)
             def _():
                 with NS("cdown"):
                     c_down(z + k, peers[j]).wait_recv()
-                c_forward(z + k, peers[j], False, has_down)
+                c_forward(z + k, j, False, has_down)
 
             if j == 1 and k + 1 < nz:
                 both(k + 1, relay)
 
             def near(l):
-                for i in range(2):
-                    c_pair_in(l, peers[i]).wait_recv()
-                a_x_in(l, 1).wait_recv()
-                accumulate(l, 2 * py, 2, False)
-
-            if j == 2:
+                c_pairs(l, 2, l).wait_recv()
+                rest_in(l).wait_recv()
+                with NS("near"):
+                    accumulate(l, 2 * py, 2, False)
+
+            if j == 1:
                 both(k, lambda l: pl.when(l == last)(lambda: near(l)))
 
         def finish(l):
@@ -380,17 +395,12 @@
 
                 @pl.when(l == last)
                 def _():
-                    for j in range(2, ndp):
-                        c_pair_in(l, peers[j]).wait_recv()
-                    a_y_in(l, 0).wait_recv()
-                    r_y_in(l).wait_recv()
-                    r_x_in(l).wait_recv()
+                    c_pairs(l, ndp - 2, nz).wait_recv()
 
                 @pl.when(l != last)
                 def _():
-                    for j in range(ndp):
-                        c_pair_in(l, peers[j]).wait_recv()
-                    a_arrived(l)
+                    c_pairs(l, ndp, l).wait_recv()
+                    rest_in(l).wait_recv()
 
             @pl.when(l != last)
             def _():
@@ -399,37 +409,8 @@
 
         both(k, finish)
 
-    @pl.loop(0, nz)
-    def _(l):
-        @pl.when(has_up & (l <= z))
-        def _():
-            for h in range(2):
-                a_up(l, h).wait_send()
-            for d in range(ndp):
-                c_up(l, d).wait_send()
-
-        @pl.when(has_down & (l >= z))
-        def _():
-            for h in range(2):
-                a_down(l, h).wait_send()
-            for d in range(ndp):
-                c_down(l, d).wait_send()
-
-        for h in range(2):
-            a_x(l, h).wait_send()
-            a_y(l, h).wait_send()
-        r_x(l).wait_send()
-        r_y(l).wait_send()
-        for k in range(1, ndp):
-            c_pair(l, peers[k]).wait_send()
-
-        @pl.when(l != z)
-        def _():
-            c_pair(l, dp).wait_send()
-
-    for k in range(1, ndp):
-        c_plane(k).wait_send()
-    c_rows().wait_send()
+    with NS("pairs"):
+        c_pairs(last, ndp, last).wait_send()
 
 
 def finishing(nz, ndp, blk_i, agrad_i, acc, a_v, cot_v, blk_o, agrad_o, wgrad_o, out_v, s, o_s):
@@ -473,6 +454,8 @@
     tok, heads = attn_out.shape
     half, width = residual.shape
     cols = width // ndp
+    if cols != heads:
+        return per_device(attn_out, out_weight, residual, target, norm_gain)
     chunk = 512 if width % 512 == 0 else 128
     chunks = width // chunk
     tiles = heads // 256 if heads % 256 == 0 else 1
@@ -501,12 +484,9 @@
             pltpu.VMEM((half, width), bf16),
             pltpu.VMEM((half, width), bf16),
             pltpu.VMEM((1, width), f32),
-            dma((4,)), dma((chunks,)), dma((chunks,)), dma((chunks,)),
-            dma((nz, 2)), dma((nz, 2)), dma((nz, 2)),
-            dma((nz, 2)), dma((nz, 2)), dma((nz, 2)), dma((nz, 2)),
-            dma((nz,)), dma((nz,)), dma((nz,)), dma((nz,)),
-            dma((ndp,)), dma((1,)), dma((1,)),
-            dma((nz, ndp)), dma((nz, ndp)), dma((nz, ndp)), dma((nz, ndp)), dma((nz, ndp)),
+            dma((3,)), dma((chunks // (2 if chunks % 2 == 0 else 1),)), dma((1,)), dma((1,)),
+            dma((nz,)), dma((nz,)), dma((nz, 2)), dma((nz,)), dma((nz,)), dma((nz,)), dma((nz,)),
+            dma((1,)), dma((1,)), dma((1,)), dma((nz, ndp)), dma((nz,)), dma((nz + 1,)),
         ],
         compiler_params=pltpu.CompilerParams(
             collective_id=0, has_side_effects=True, vmem_limit_bytes=34 * 1000 * 1000

time: 89.9 us -> 88.5 us (0.984)
  Pallas kernels: 89 us -> 87.7 us
    pallas_call x1, Pallas kernels: 84.9 us -> 83.6 us  [fused_device(): pl.pallas_call(functools.partial(fused, nz, ndp, chunk), out_shape=(pltpu...]
where the time goes in v2:
time: 88.5 us; the launch traced here: 88.3 us
  Pallas kernels  87.7 us (99%)
    pallas_call x1, Pallas kernels, fused_device(): pl.pallas_call(functools.partial(fused, nz, ndp, chunk), out_shape=(pltpu...  83.6 us
    pallas_call x1, Pallas kernels, fused_device(): pl.pallas_call(functools.partial(finishing, nz, ndp), out_shape=(jax.Shap...  4.08 us

profile of v2, /device:TPU:0, one launch (start us, length us, event | category | flops | bytes accessed | tf_op | source)
XLA Modules:
  0.0 88.3 jit_solution(6726458929794389022)
XLA Ops:
  0.6 83.6 %shard_map.76 = (bf16[64,6144]{1,0:T(8,128)(2,1)S(1)}, bf16[128,1536]{1,0:T(8,128)(2,1)S(1)}, f32[1536,1536]{1,0:T(8,128)S(1)}, bf16[4,4,128,1536]{3,2,1,0:T(8,128)(2,1)S(1)}, bf16[4,4,2,64,1536]{4,3,2,1,0:T(8,128)(2,1)S(1)}) custom-call(bf16[128,1536]{1,0:T(8,128)(2,1)} %attn_h.1, bf16[1536,6144]{1,0:T(8,128)(2,1)} %w_h.1, bf16[64,6144]{1,0:T(8,128)(2,1)} %res_h.1, ...), custom_call_target="tpu_custom_call" | custom-call | tf_op jit(solution)/shard_map/pallas_call | solution.py:468
  84.2 4.1 %shard_map.77 = (bf16[64,6144]{1,0:T(8,128)(2,1)}, bf16[128,1536]{1,0:T(8,128)(2,1)}, f32[1536,1536]{1,0:T(8,128)}) custom-call(bf16[64,6144]{1,0:T(8,128)(2,1)S(1)} %get-tuple-element.8.blk_i, bf16[128,1536]{1,0:T(8,128)(2,1)S(1)} %get-tuple-element.9.agrad_i, f32[1536,1536]{1,0:T(8,128)S(1)} %get-tuple-element.10.acc, ...), custom_call_target="tpu_custom_call" | custom-call | tf_op jit(solution)/shard_map/pallas_call | solution.py:495

commit v3 on v2

--- a/solution.py
+++ b/solution.py
@@ -61,6 +61,7 @@
 
 
 NS = jax.named_scope
+HEAD = 3
 MESH = pl.DeviceIdType.MESH
 
 
@@ -77,7 +78,7 @@
 def fused(
     nz, ndp, chunk, attn_h, w_h, res_h, tgt_h, gain_h, blk_v, agrad_v, acc, a_v, cot_v,
     w_v, rows_v, part, part_in, res_v, tgt_v, gain_v,
-    ld_s, w_s, p_s, p_r, up_s, dn_s, az_r, pl_s, fx_r, fy_r, pl_r, cp_s, cq_s, cq_r, c_r, ce_s, ce_r,
+    near_s, ready_s, ld_s, w_s, p_s, p_r, up_s, dn_s, az_r, pl_s, fx_r, fy_r, pl_r, cp_s, cq_s, cq_r, c_r, ce_s, ce_r,
 ):
     z, dp, m = lax.axis_index("cuts"), lax.axis_index("dp"), lax.axis_index("mp")
     other = 1 - m
@@ -104,27 +105,21 @@
         at = pl.ds(pl.multiple_of(c * per_load * chunk, chunk), per_load * chunk)
         return pltpu.make_async_copy(w_h.at[:, at], w_v.at[:, at], w_s.at[c])
 
+    is_end = (z == 0) | (z == nz - 1)
     barrier = pltpu.get_barrier_semaphore()
+    pl.when(has_up)(lambda: pl.semaphore_signal(barrier, inc=1, device_id={"cuts": z + 1}, device_id_type=MESH))
+    pl.when(has_down)(lambda: pl.semaphore_signal(barrier, inc=1, device_id={"cuts": z - 1}, device_id_type=MESH))
     pl.semaphore_signal(barrier, inc=1, device_id={"mp": other}, device_id_type=MESH)
-    for peer in peers[1:]:
-        pl.semaphore_signal(barrier, inc=1, device_id={"dp": peer}, device_id_type=MESH)
-
-    @pl.when(has_up)
+
+    @pl.when(is_end)
     def _():
-        pl.semaphore_signal(barrier, inc=1, device_id={"cuts": z + 1}, device_id_type=MESH)
-
-    @pl.when(has_down)
-    def _():
-        pl.semaphore_signal(barrier, inc=1, device_id={"cuts": z - 1}, device_id_type=MESH)
+        for peer in (xn, yn):
+            pl.semaphore_signal(barrier, inc=1, device_id={"dp": peer}, device_id_type=MESH)
 
     with NS("aload"):
         a_load.wait()
-    for c in range(chunks // per_load):
-        w_load(c).start()
-    for load in loads:
-        load.start()
     with NS("barrier"):
-        pl.semaphore_wait(barrier, ndp + jnp.where(has_up, 1, 0) + jnp.where(has_down, 1, 0))
+        pl.semaphore_wait(barrier, jnp.where(is_end, 4, 3))
 
     def rows(h):
         return pl.ds(h * half, half)
@@ -218,7 +213,31 @@
     for h in range(2):
         pl.when(has_up)(lambda: a_up(z, h).start())
         pl.when(has_down)(lambda: a_down(z, h).start())
-    a_plane(z)
+    for c in range(chunks // per_load):
+        w_load(c).start()
+    for load in loads:
+        load.start()
+
+    @pl.when(is_end)
+    def _():
+        a_plane(z)
+        for peer in (xn, yn):
+            pl.semaphore_signal(near_s, inc=1, device_id={"dp": peer}, device_id_type=MESH)
+        with NS("near_s"):
+            pl.semaphore_wait(near_s, 2)
+
+        @pl.when((z == 0) & (nz > 2))
+        def _():
+            pl.semaphore_signal(ready_s, inc=1, device_id={"cuts": z + 1}, device_id_type=MESH)
+
+        @pl.when((z == nz - 1) & (nz > 3))
+        def _():
+            pl.semaphore_signal(ready_s, inc=1, device_id={"cuts": z - 1}, device_id_type=MESH)
+
+    def a_middle():
+        with NS("ready_s"):
+            pl.semaphore_wait(ready_s, 1)
+        a_plane(z)
 
     def p_send(c):
         at = pl.ds(pl.multiple_of(c * chunk, chunk), chunk)
@@ -228,6 +247,7 @@
     def _(c):
         at = pl.ds(pl.multiple_of(c * chunk, chunk), chunk)
         pl.when(lax.rem(c, per_load) == 0)(lambda: w_load(lax.div(c, per_load)).wait())
+        pl.when(jnp.logical_not(is_end) & (c == min(HEAD, chunks - 1)))(a_middle)
         value = jnp.dot(a_v[z, dp], w_v[:, at], preferred_element_type=jnp.float32).astype(jnp.bfloat16)
         part[0, :, at] = value[:half]
         part[1, :, at] = value[half:]
@@ -356,6 +376,25 @@
         c_rows().wait_send()
 
     both(1, relay)
+    def near(l):
+        c_pairs(l, 2, l).wait_recv()
+        rest_in(l).wait_recv()
+        with NS("near"):
+            accumulate(l, 2 * py, 2, False)
+
+    def finish(l):
+        @pl.when(l == last)
+        def _():
+            c_pairs(l, ndp - 2, nz).wait_recv()
+
+        @pl.when(l != last)
+        def _():
+            with NS("cpair"):
+                c_pairs(l, ndp, l).wait_recv()
+                rest_in(l).wait_recv()
+            with NS("group"):
+                accumulate(l, 0, ndp, False)
+
     for k in range(1, nz):
         if k == nz - 1:
             with NS("drain"):
@@ -378,36 +417,19 @@
                     c_down(z + k, peers[j]).wait_recv()
                 c_forward(z + k, j, False, has_down)
 
-            if j == 1 and k + 1 < nz:
+            if j == ndp - 2 and k + 1 < nz:
                 both(k + 1, relay)
-
-            def near(l):
-                c_pairs(l, 2, l).wait_recv()
-                rest_in(l).wait_recv()
-                with NS("near"):
-                    accumulate(l, 2 * py, 2, False)
-
             if j == 1:
-                both(k, lambda l: pl.when(l == last)(lambda: near(l)))
-
-        def finish(l):
-            with NS("cpair"):
-
-                @pl.when(l == last)
-                def _():
-                    c_pairs(l, ndp - 2, nz).wait_recv()
-
-                @pl.when(l != last)
-                def _():
-                    c_pairs(l, ndp, l).wait_recv()
-                    rest_in(l).wait_recv()
-
-            @pl.when(l != last)
+                both(k, lambda l: pl.when(is_end & (l == last))(lambda: near(l)))
+
+        both(k, lambda l: pl.when(is_end)(lambda: finish(l)))
+        if k == nz - 2:
+
+            @pl.when(jnp.logical_not(is_end))
             def _():
-                with NS("group"):
-                    accumulate(l, 0, ndp, False)
-
-        both(k, finish)
+                for i in range(1, nz - 1):
+                    both(i, lambda l: pl.when(l == last)(lambda: near(l)))
+                    both(i, finish)
 
     with NS("pairs"):
         c_pairs(last, ndp, last).wait_send()
@@ -484,7 +506,7 @@
             pltpu.VMEM((half, width), bf16),
             pltpu.VMEM((half, width), bf16),
             pltpu.VMEM((1, width), f32),
-            dma((3,)), dma((chunks // (2 if chunks % 2 == 0 else 1),)), dma((1,)), dma((1,)),
+            pltpu.SemaphoreType.REGULAR, pltpu.SemaphoreType.REGULAR, dma((3,)), dma((chunks // (2 if chunks % 2 == 0 else 1),)), dma((1,)), dma((1,)),
             dma((nz,)), dma((nz,)), dma((nz, 2)), dma((nz,)), dma((nz,)), dma((nz,)), dma((nz,)),
             dma((1,)), dma((1,)), dma((1,)), dma((nz, ndp)), dma((nz,)), dma((nz + 1,)),
         ],
@@ -507,7 +529,7 @@
 
 
 def solution(mesh):
-    if mesh.shape["mp"] == 2 and mesh.shape["dp"] == 4 and mesh.shape["cuts"] > 1:
+    if mesh.shape["mp"] == 2 and mesh.shape["dp"] == 4 and 1 < mesh.shape["cuts"] < 5:
         body = functools.partial(fused_device, mesh.shape["cuts"], mesh.shape["dp"])
     else:
         body = per_device

time: 88.5 us -> 87.5 us (0.989)
  Pallas kernels: 87.7 us -> 86.7 us
    pallas_call x1, Pallas kernels: 83.6 us -> 82.6 us  [fused_device(): pl.pallas_call(functools.partial(fused, nz, ndp, chunk), out_shape=(pltpu...]
where the time goes in v3:
time: 87.5 us; the launch traced here: 87.4 us
  Pallas kernels  86.7 us (99%)
    pallas_call x1, Pallas kernels, fused_device(): pl.pallas_call(functools.partial(fused, nz, ndp, chunk), out_shape=(pltpu...  82.6 us
    pallas_call x1, Pallas kernels, fused_device(): pl.pallas_call(functools.partial(finishing, nz, ndp), out_shape=(jax.Shap...  4.08 us

profile of v3, /device:TPU:0, one launch (start us, length us, event | category | flops | bytes accessed | tf_op | source)
XLA Modules:
  0.0 87.4 jit_solution(6661085044403429860)
XLA Ops:
  0.6 82.6 %shard_map.76 = (bf16[64,6144]{1,0:T(8,128)(2,1)S(1)}, bf16[128,1536]{1,0:T(8,128)(2,1)S(1)}, f32[1536,1536]{1,0:T(8,128)S(1)}, bf16[4,4,128,1536]{3,2,1,0:T(8,128)(2,1)S(1)}, bf16[4,4,2,64,1536]{4,3,2,1,0:T(8,128)(2,1)S(1)}) custom-call(bf16[128,1536]{1,0:T(8,128)(2,1)} %attn_h.1, bf16[1536,6144]{1,0:T(8,128)(2,1)} %w_h.1, bf16[64,6144]{1,0:T(8,128)(2,1)} %res_h.1, ...), custom_call_target="tpu_custom_call" | custom-call | tf_op jit(solution)/shard_map/pallas_call | solution.py:490
  83.3 4.1 %shard_map.77 = (bf16[64,6144]{1,0:T(8,128)(2,1)}, bf16[128,1536]{1,0:T(8,128)(2,1)}, f32[1536,1536]{1,0:T(8,128)}) custom-call(bf16[64,6144]{1,0:T(8,128)(2,1)S(1)} %get-tuple-element.8.blk_i, bf16[128,1536]{1,0:T(8,128)(2,1)S(1)} %get-tuple-element.9.agrad_i, f32[1536,1536]{1,0:T(8,128)S(1)} %get-tuple-element.10.acc, ...), custom_call_target="tpu_custom_call" | custom-call | tf_op jit(solution)/shard_map/pallas_call | solution.py:517

commit v4 on v3

--- a/solution.py
+++ b/solution.py
@@ -78,7 +78,7 @@
 def fused(
     nz, ndp, chunk, attn_h, w_h, res_h, tgt_h, gain_h, blk_v, agrad_v, acc, a_v, cot_v,
     w_v, rows_v, part, part_in, res_v, tgt_v, gain_v,
-    near_s, ready_s, ld_s, w_s, p_s, p_r, up_s, dn_s, az_r, pl_s, fx_r, fy_r, pl_r, cp_s, cq_s, cq_r, c_r, ce_s, ce_r,
+    ready_s, above_s, ld_s, w_s, p_r, up_s, dn_s, az_r, pl_s, fx_r, fy_r, pl_r, cq_r, c_r, cx_r, ce_r,
 ):
     z, dp, m = lax.axis_index("cuts"), lax.axis_index("dp"), lax.axis_index("mp")
     other = 1 - m
@@ -106,9 +106,15 @@
         return pltpu.make_async_copy(w_h.at[:, at], w_v.at[:, at], w_s.at[c])
 
     is_end = (z == 0) | (z == nz - 1)
+    second = (z == 1) if nz == 4 else (z < 0)
+    third = (z == 2) if nz == 4 else (z < 0)
     barrier = pltpu.get_barrier_semaphore()
     pl.when(has_up)(lambda: pl.semaphore_signal(barrier, inc=1, device_id={"cuts": z + 1}, device_id_type=MESH))
-    pl.when(has_down)(lambda: pl.semaphore_signal(barrier, inc=1, device_id={"cuts": z - 1}, device_id_type=MESH))
+
+    @pl.when(has_down & jnp.logical_not(third))
+    def _():
+        pl.semaphore_signal(barrier, inc=1, device_id={"cuts": z - 1}, device_id_type=MESH)
+
     pl.semaphore_signal(barrier, inc=1, device_id={"mp": other}, device_id_type=MESH)
 
     @pl.when(is_end)
@@ -119,7 +125,7 @@
     with NS("aload"):
         a_load.wait()
     with NS("barrier"):
-        pl.semaphore_wait(barrier, jnp.where(is_end, 4, 3))
+        pl.semaphore_wait(barrier, jnp.where(is_end, 4, jnp.where(second, 2, 3)))
 
     def rows(h):
         return pl.ds(h * half, half)
@@ -134,25 +140,25 @@
         return remote(piece(l, dp, h), piece(l, dp, h), dn_s.at[l], az_r.at[l, h], cuts=z - 1)
 
     def a_x(l, h):
-        return remote(piece(l, dp, h), piece(l, dp, h), pl_s.at[l], (fx_r if h == 0 else pl_r).at[l], dp=xn)
+        return remote(piece(l, dp, h), piece(l, dp, h), pl_s.at[0], (fx_r if h == 0 else pl_r).at[l], dp=xn)
 
     def a_y(l, h):
-        return remote(piece(l, dp, h), piece(l, dp, h), pl_s.at[l], (fy_r if h == 1 else pl_r).at[l], dp=yn)
+        return remote(piece(l, dp, h), piece(l, dp, h), pl_s.at[0], (fy_r if h == 1 else pl_r).at[l], dp=yn)
 
     def first_x_in(l):
-        return remote(piece(l, xn, 0), piece(l, xn, 0), pl_s.at[l], fx_r.at[l], dp=xn)
+        return remote(piece(l, xn, 0), piece(l, xn, 0), pl_s.at[0], fx_r.at[l], dp=xn)
 
     def first_y_in(l):
-        return remote(piece(l, yn, 1), piece(l, yn, 1), pl_s.at[l], fy_r.at[l], dp=yn)
+        return remote(piece(l, yn, 1), piece(l, yn, 1), pl_s.at[0], fy_r.at[l], dp=yn)
 
     def r_y(l):
-        return remote(piece(l, xn, 0), piece(l, xn, 0), pl_s.at[l], pl_r.at[l], dp=yn)
+        return remote(piece(l, xn, 0), piece(l, xn, 0), pl_s.at[0], pl_r.at[l], dp=yn)
 
     def r_x(l):
-        return remote(piece(l, yn, 1), piece(l, yn, 1), pl_s.at[l], pl_r.at[l], dp=xn)
+        return remote(piece(l, yn, 1), piece(l, yn, 1), pl_s.at[0], pl_r.at[l], dp=xn)
 
     def rest_in(l):
-        return remote(a_v.at[l, :2], a_v.at[l, :2], pl_s.at[l], pl_r.at[l], dp=xn)
+        return remote(a_v.at[l, :2], a_v.at[l, :2], pl_s.at[0], pl_r.at[l], dp=xn)
 
     def sent_up(l):
         return remote(a_v.at[l, :3], a_v.at[l, :3], up_s.at[l], pl_r.at[l], cuts=z + 1)
@@ -160,8 +166,8 @@
     def sent_down(l):
         return remote(a_v.at[l, :3], a_v.at[l, :3], dn_s.at[l], pl_r.at[l], cuts=z - 1)
 
-    def sent_plane(l):
-        return remote(a_v.at[l, :3], a_v.at[l, :3], pl_s.at[l], pl_r.at[l], dp=xn)
+    def sent_plane():
+        return remote(a_v.at[:, :3], a_v.at[:, :3], pl_s.at[0], pl_r.at[0], dp=xn)
 
     def c_up(l, d, src=None):
         return remote(cot_v.at[l, d, m] if src is None else src, cot_v.at[l, d, m], up_s.at[l], c_r.at[l, d], cuts=z + 1)
@@ -169,12 +175,23 @@
     def c_down(l, d, src=None):
         return remote(cot_v.at[l, d, m] if src is None else src, cot_v.at[l, d, m], dn_s.at[l], c_r.at[l, d], cuts=z - 1)
 
+    def cut(i):
+        return pl.ds(0, half - 16) if i == 0 else pl.ds(half - 16, 16)
+
+    def c_cut(l, i, sem, to):
+        block = cot_v.at[l, dg, m, cut(i)]
+        return remote(block, block, sem, c_r.at[l, dg] if i == 0 else cx_r.at[0], cuts=to)
+
+    def c_pair_cut(l, i):
+        block = cot_v.at[l, dg, m, cut(i)]
+        return remote(block, block, w_s.at[l], ce_r.at[nz], mp=other)
+
     def c_pair(l, d, group):
-        return remote(cot_v.at[l, d, m], cot_v.at[l, d, m], ce_s.at[l], ce_r.at[group], mp=other)
+        return remote(cot_v.at[l, d, m], cot_v.at[l, d, m], w_s.at[l], ce_r.at[group], mp=other)
 
     def c_pairs(l, count, group):
         blocks = cot_v.at[l, :count, other]
-        return remote(blocks, blocks, ce_s.at[l], ce_r.at[group], mp=other)
+        return remote(blocks, blocks, w_s.at[l], ce_r.at[group], mp=other)
 
     def both(k, f):
         pl.when(z - k >= 0)(lambda: f(z - k))
@@ -211,8 +228,19 @@
         r_x(l).start()
 
     for h in range(2):
-        pl.when(has_up)(lambda: a_up(z, h).start())
+        pl.when(has_up & jnp.logical_not(second))(lambda: a_up(z, h).start())
         pl.when(has_down)(lambda: a_down(z, h).start())
+
+    @pl.when(third)
+    def _():
+        pl.semaphore_signal(above_s, inc=1, device_id={"cuts": z - 1}, device_id_type=MESH)
+
+    def a_second():
+        with NS("above_s"):
+            pl.semaphore_wait(above_s, 1)
+        for h in range(2):
+            a_up(z, h).start()
+
     for c in range(chunks // per_load):
         w_load(c).start()
     for load in loads:
@@ -222,9 +250,9 @@
     def _():
         a_plane(z)
         for peer in (xn, yn):
-            pl.semaphore_signal(near_s, inc=1, device_id={"dp": peer}, device_id_type=MESH)
+            pl.semaphore_signal(ready_s, inc=1, device_id={"dp": peer}, device_id_type=MESH)
         with NS("near_s"):
-            pl.semaphore_wait(near_s, 2)
+            pl.semaphore_wait(ready_s, 2)
 
         @pl.when((z == 0) & (nz > 2))
         def _():
@@ -241,12 +269,13 @@
 
     def p_send(c):
         at = pl.ds(pl.multiple_of(c * chunk, chunk), chunk)
-        return remote(part.at[other, :, at], part_in.at[:, at], p_s.at[0], p_r.at[0], mp=other)
+        return remote(part.at[other, :, at], part_in.at[:, at], ld_s.at[0], p_r.at[0], mp=other)
 
     @pl.loop(0, chunks)
     def _(c):
         at = pl.ds(pl.multiple_of(c * chunk, chunk), chunk)
         pl.when(lax.rem(c, per_load) == 0)(lambda: w_load(lax.div(c, per_load)).wait())
+        pl.when(second & (c == min(1, chunks - 1)))(a_second)
         pl.when(jnp.logical_not(is_end) & (c == min(HEAD, chunks - 1)))(a_middle)
         value = jnp.dot(a_v[z, dp], w_v[:, at], preferred_element_type=jnp.float32).astype(jnp.bfloat16)
         part[0, :, at] = value[:half]
@@ -260,7 +289,7 @@
         loads[2].wait()
 
     with NS("psend"):
-        remote(part_in, part_in, p_s.at[0], p_r.at[0], mp=other).wait()
+        remote(part_in, part_in, ld_s.at[0], p_r.at[0], mp=other).wait()
 
     step = 16
     gain = gain_v[...]
@@ -286,13 +315,13 @@
             rows_v[d, m, at, :] = cot[:, d * cols : (d + 1) * cols]
 
     def c_plane(k):
-        return remote(rows_v.at[peers[k], m], cot_v.at[z, dp, m], cp_s.at[0], c_r.at[z, dp], dp=peers[k])
+        return remote(rows_v.at[peers[k], m], cot_v.at[z, dp, m], w_s.at[nz], c_r.at[z, dp], dp=peers[k])
 
     def c_rows():
-        return remote(rows_v.at[:, m], rows_v.at[:, m], cq_s.at[0], cq_r.at[0], mp=other)
+        return remote(rows_v.at[:, m], rows_v.at[:, m], w_s.at[nz + 1], cq_r.at[0], mp=other)
 
     def c_rows_in():
-        return remote(rows_v.at[:, other], rows_v.at[:, other], cq_s.at[0], cq_r.at[0], mp=other)
+        return remote(rows_v.at[:, other], rows_v.at[:, other], w_s.at[nz + 1], cq_r.at[0], mp=other)
 
     own = rows_v.at[dp, m]
     pl.when(has_up)(lambda: c_up(z, dp, own).start())
@@ -320,9 +349,14 @@
             )
         agrad_v[:, at] = total.astype(jnp.bfloat16)
 
-    def c_forward(l, j, up, down):
-        pl.when(up)(lambda: c_up(l, peers[j]).start())
-        pl.when(down)(lambda: c_down(l, peers[j]).start())
+    def c_forward(l, j, up, down, pieces=False):
+        if pieces:
+            for i in range(2):
+                pl.when(up)(lambda: c_cut(l, i, up_s.at[l], z + 1).start())
+                pl.when(down)(lambda: c_cut(l, i, dn_s.at[l], z - 1).start())
+        else:
+            pl.when(up)(lambda: c_up(l, peers[j]).start())
+            pl.when(down)(lambda: c_down(l, peers[j]).start())
         c_pair(l, peers[j], l if j < 2 else jnp.where(l == last, nz, l)).start()
 
     tiles = heads // tile
@@ -364,15 +398,15 @@
         def _(l):
             pl.when(has_up & (l <= z))(lambda: sent_up(l).wait_send())
             pl.when(has_down & (l >= z))(lambda: sent_down(l).wait_send())
-            sent_plane(l).wait_send()
 
             @pl.when((l != last) & (l != z))
             def _():
                 c_pairs(l, ndp, l).wait_send()
 
+        sent_plane().wait_send()
         c_pairs(z, ndp - 1, z).wait_send()
         blocks = cot_v.at[z, : ndp - 1, m]
-        remote(blocks, blocks, cp_s.at[0], c_r.at[z, dp], dp=xn).wait_send()
+        remote(blocks, blocks, w_s.at[nz], c_r.at[z, dp], dp=xn).wait_send()
         c_rows().wait_send()
 
     both(1, relay)
@@ -404,18 +438,30 @@
         if k + 2 < nz:
             both(k + 2, a_plane)
         for j in range(ndp):
+            pieces = k == nz - 2 and j == ndp - 1
+
+            if k == nz - 1 and j == ndp - 1:
+
+                @pl.when(is_end)
+                def _():
+                    for i in range(2):
+                        with NS("cut"):
+                            c_cut(last, i, up_s.at[last], z).wait_recv()
+                        c_pair_cut(last, i).start()
+
+                continue
 
             @pl.when(z - k >= 0)
             def _():
                 with NS("cup"):
                     c_up(z - k, peers[j]).wait_recv()
-                c_forward(z - k, j, has_up, False)
+                c_forward(z - k, j, has_up, False, pieces)
 
             @pl.when(z + k < nz)
             def _():
                 with NS("cdown"):
                     c_down(z + k, peers[j]).wait_recv()
-                c_forward(z + k, j, False, has_down)
+                c_forward(z + k, j, False, has_down, pieces)
 
             if j == ndp - 2 and k + 1 < nz:
                 both(k + 1, relay)
@@ -506,9 +552,9 @@
             pltpu.VMEM((half, width), bf16),
             pltpu.VMEM((half, width), bf16),
             pltpu.VMEM((1, width), f32),
-            pltpu.SemaphoreType.REGULAR, pltpu.SemaphoreType.REGULAR, dma((3,)), dma((chunks // (2 if chunks % 2 == 0 else 1),)), dma((1,)), dma((1,)),
-            dma((nz,)), dma((nz,)), dma((nz, 2)), dma((nz,)), dma((nz,)), dma((nz,)), dma((nz,)),
-            dma((1,)), dma((1,)), dma((1,)), dma((nz, ndp)), dma((nz,)), dma((nz + 1,)),
+            pltpu.SemaphoreType.REGULAR, pltpu.SemaphoreType.REGULAR, dma((3,)), dma((max(nz + 2, chunks // (2 if chunks % 2 == 0 else 1)),)), dma((1,)),
+            dma((nz,)), dma((nz,)), dma((nz, 2)), dma((1,)), dma((nz,)), dma((nz,)), dma((nz,)),
+            dma((1,)), dma((nz, ndp)), dma((1,)), dma((nz + 1,)),
         ],
         compiler_params=pltpu.CompilerParams(
             collective_id=0, has_side_effects=True, vmem_limit_bytes=34 * 1000 * 1000
@@ -529,7 +575,7 @@
 
 
 def solution(mesh):
-    if mesh.shape["mp"] == 2 and mesh.shape["dp"] == 4 and 1 < mesh.shape["cuts"] < 5:
+    if mesh.shape["mp"] == 2 and mesh.shape["dp"] == 4 and 2 < mesh.shape["cuts"] < 5:
         body = functools.partial(fused_device, mesh.shape["cuts"], mesh.shape["dp"])
     else:
         body = per_device

time: 87.5 us -> 86.9 us (level)
  no operation moved by 1% of the time
where the time goes in v4:
time: 86.9 us; the launch traced here: 86.8 us
  Pallas kernels  86.1 us (99%)
    pallas_call x1, Pallas kernels, fused_device(): pl.pallas_call(functools.partial(fused, nz, ndp, chunk), out_shape=(pltpu...  82.1 us
    pallas_call x1, Pallas kernels, fused_device(): pl.pallas_call(functools.partial(finishing, nz, ndp), out_shape=(jax.Shap...  4.08 us

profile of v4, /device:TPU:0, one launch (start us, length us, event | category | flops | bytes accessed | tf_op | source)
XLA Modules:
  0.0 86.8 jit_solution(7829678586139205807)
XLA Ops:
  0.6 82.1 %shard_map.76 = (bf16[64,6144]{1,0:T(8,128)(2,1)S(1)}, bf16[128,1536]{1,0:T(8,128)(2,1)S(1)}, f32[1536,1536]{1,0:T(8,128)S(1)}, bf16[4,4,128,1536]{3,2,1,0:T(8,128)(2,1)S(1)}, bf16[4,4,2,64,1536]{4,3,2,1,0:T(8,128)(2,1)S(1)}) custom-call(bf16[128,1536]{1,0:T(8,128)(2,1)} %attn_h.1, bf16[1536,6144]{1,0:T(8,128)(2,1)} %w_h.1, bf16[64,6144]{1,0:T(8,128)(2,1)} %res_h.1, ...), custom_call_target="tpu_custom_call" | custom-call | tf_op jit(solution)/shard_map/pallas_call | solution.py:536
  82.7 4.1 %shard_map.77 = (bf16[64,6144]{1,0:T(8,128)(2,1)}, bf16[128,1536]{1,0:T(8,128)(2,1)}, f32[1536,1536]{1,0:T(8,128)}) custom-call(bf16[64,6144]{1,0:T(8,128)(2,1)S(1)} %get-tuple-element.8.blk_i, bf16[128,1536]{1,0:T(8,128)(2,1)S(1)} %get-tuple-element.9.agrad_i, f32[1536,1536]{1,0:T(8,128)S(1)} %get-tuple-element.10.acc, ...), custom_call_target="tpu_custom_call" | custom-call | tf_op jit(solution)/shard_map/pallas_call | solution.py:563
